TPU v7x, 256 devices: a whole 4x4x8 slice. The times are simulated.
256 devices in a mesh: gx: 8 (over z), gy: 16 (over x, y), gz: 2 (over core).
Axes of the slice: x: 4, y: 4, z: 8, core: 2. Of those that a mesh axis runs over, the one named last changes fastest.
Arguments:
- panels: float32 [4, 32768], P(None, ('gy', 'gz')), may hold values from -2 to 3, as said below
- diagonal: float32 [32768], P(('gy', 'gz')), may hold values from 0.5 to 2
- right_side: float32 [32, 32768], P(None, ('gy', 'gz')), may hold values from -6 to 6
- start_guess: float32 [32, 32768], P(None, ('gy', 'gz')), may hold values from -6 to 6
Outputs:
- solution: float32 [32, 32768], P(None, ('gy', 'gz'))
- residual: float32 [32, 32768], P(None, ('gy', 'gz'))
- history: float32 [4, 32], replicated
Inputs may be any that keep to these rules, and one draw needn't show every extreme that they name: `panels`: rows 0 to 2 are centroids of a closed surface around the anchor, row 3 positive areas between 0.3 and 3.
All inputs are finite; a program needn't handle non-finite values.
Results may differ from a plain program's by a relative error of at most 0.00035.
Values sent between devices are 32-bit elements; how exact they have to be, the bound alone decides.
A program may use at most 64 MiB of HBM per device.

v0:
```python
import jax
import jax.numpy as jnp
from jax import lax
from jax.sharding import PartitionSpec as P

N = 32768
ITERS = 4


soft_sq = 0.0025


def from_root(shard, axis, root):
    return lax.dynamic_index_in_dim(lax.all_gather(shard, axis), root, 0, keepdims=False)


def from_everyone(shard, axis):
    copies = jnp.broadcast_to(shard, (lax.axis_size(axis), *shard.shape))
    return lax.all_to_all(copies, axis, split_axis=0, concat_axis=0, tiled=True)


def over_copies(shard, axis):
    return from_everyone(shard, axis).sum(axis=0)


def kernel(row_pan, col_pan):
    dist_sq = (row_pan[0][:, None] - col_pan[0][None, :]) ** 2
    dist_sq = dist_sq + (row_pan[1][:, None] - col_pan[1][None, :]) ** 2
    dist_sq = dist_sq + (row_pan[2][:, None] - col_pan[2][None, :]) ** 2
    weight = (row_pan[3] * N ** (-0.5))[:, None] * col_pan[3][None, :]
    return weight * lax.rsqrt(dist_sq + soft_sq)


def on_device(panels, diagonal, right_side, start_guess):
    col_count = panels.shape[1]
    cases = right_side.shape[0]
    row_len = N // lax.axis_size("gx")
    per_row = row_len // col_count
    row_index = lax.axis_index("gx")
    pan_pieces = []
    for piece_index in range(per_row):
        pan_pieces.append(from_root(panels, ("gy", "gz"), row_index * per_row + piece_index))
    row_pan = jnp.concatenate(pan_pieces, 1)
    kernel_block = kernel(row_pan, panels)

    def matvec(vector):
        vec_pieces = []
        for piece_index in range(per_row):
            vec_pieces.append(from_root(vector, ("gy", "gz"), row_index * per_row + piece_index))
        row_part = jnp.concatenate(vec_pieces, 1)
        partial_value = jnp.dot(row_part, kernel_block, precision=lax.Precision.HIGHEST)
        summed = over_copies(partial_value, "gx")
        return diagonal[None, :] * vector + summed

    residual = right_side - matvec(start_guess)
    image_res = matvec(residual)
    solution = start_guess
    direction = jnp.zeros_like(residual)
    sdir = jnp.zeros_like(residual)
    zdir = jnp.zeros_like(residual)
    gamma_prev = jnp.ones((cases,), jnp.float32)
    alpha_prev = jnp.ones((cases,), jnp.float32)
    records = []
    for turn_index in range(ITERS):
        fresh = matvec(image_res)
        gamma_now, delta_now, omega_now = jax.tree.map(
            lambda part: over_copies(part, ("gy", "gz")),
            (
                jnp.sum(residual * residual, 1),
                jnp.sum(image_res * residual, 1),
                jnp.sum(image_res * image_res, 1),
            ),
        )
        records.append(jnp.sqrt(omega_now / gamma_now))
        if turn_index == 0:
            beta_now = jnp.zeros((cases,), jnp.float32)
            alpha_now = gamma_now / delta_now
        else:
            beta_now = gamma_now / gamma_prev
            alpha_now = gamma_now / (delta_now - beta_now * gamma_now / alpha_prev)
        beta_col = beta_now[:, None]
        alpha_col = alpha_now[:, None]
        zdir = fresh + beta_col * zdir
        sdir = image_res + beta_col * sdir
        direction = residual + beta_col * direction
        solution = solution + alpha_col * direction
        residual = residual - alpha_col * sdir
        image_res = image_res - alpha_col * zdir
        gamma_prev = gamma_now
        alpha_prev = alpha_now
    return (solution, residual, jnp.stack(records))


def solution(mesh):
    placed = (P(None, ("gy", "gz")), P(("gy", "gz")), P(None, ("gy", "gz")), P(None, ("gy", "gz")))
    return jax.shard_map(
        on_device,
        mesh=mesh,
        in_specs=placed,
        out_specs=(P(None, ("gy", "gz")), P(None, ("gy", "gz")), P()),
        check_vma=False,
    )
```

profile of v0, /device:TPU:1, one launch (start us, length us, event | category | flops | bytes accessed | tf_op | source)
XLA Modules:
  0.0 592.2 jit_solution(13859345261153002498)
XLA Ops:
  8.0 26.4 %all-gather.6 = f32[32,4,1024]{2,1,0:T(4,128)S(1)} all-gather(f32[1,4,1024]{2,1,0:T(4,128)} %bitcast.82), channel_id=3, replica_groups=mesh['gx'=8,'gy'=16,'gz'=2] {'gy','gz'}, dimensions={0}, use_global_device_ids=true | all-gather | bytes 540672 | tf_op jit(solution)/shard_map/all_gather | solution.py:14
  35.4 30.5 %all-gather.13.cloned.1.call-done = f32[1024,1024]{1,0:T(8,128)} async-done(((f32[32,1024]{1,0:T(8,128)}), f32[1024,1024]{1,0:T(8,128)}) %all-gather.13.cloned.1.call-update) | async-done | bytes 4194320 | tf_op jit(solution)/shard_map/all_gather | solution.py:14
  67.0 17.0 %fusion.4 = f32[32,1024]{1,0:T(8,128)S(1)} fusion(f32[1024]{0:T(1024)S(1)} %bitcast.130, f32[4096]{0:T(1024)S(1)} %bitcast.105, f32[1024]{0:T(1024)S(1)} %bitcast.135, f32[4096]{0:T(1024)S(1)} %bitcast.110, f32[1024]{0:T(1024)S(1)} %bitcast.125, f32[4096]{0:T(1024)S(1)} %bitcast.115, f32[1024]{0:T(1024)S(1)} %bitcast.120, f32[4096]{0:T(1024)S(1)} %bitcast.100, ...), kind=kOutput, calls=%fused_computation.5 | convolution fusion | flops 1657143296 | bytes 737280 | tf_op jit(solution)/shard_map/dot_general | solution.py:51
  84.1 35.1 %all_to_all.97 = f32[8,32,1024]{2,1,0:T(8,128)S(1)} all-to-all(f32[8,32,1024]{2,1,0:T(8,128)S(1)} %broadcast_in_dim.64), channel_id=1, replica_groups=mesh['gx'=8,'gy'=16,'gz'=2] {'gx'}, dimensions={0} | all-to-all | bytes 2097152 | tf_op jit(solution)/shard_map/all_to_all | solution.py:19
  120.1 46.2 %all-gather.15.cloned.1.call-done = f32[1024,1024]{1,0:T(8,128)} async-done(((f32[32,1024]{1,0:T(8,128)}), f32[1024,1024]{1,0:T(8,128)}) %all-gather.15.cloned.1.call-update) | async-done | bytes 4194320 | tf_op jit(solution)/shard_map/all_gather | solution.py:14
  167.4 16.7 %fusion.3 = f32[32,1024]{1,0:T(8,128)S(1)} fusion(f32[1024]{0:T(1024)S(1)} %bitcast.131, f32[4096]{0:T(1024)S(1)} %bitcast.106, f32[1024]{0:T(1024)S(1)} %bitcast.136, f32[4096]{0:T(1024)S(1)} %bitcast.111, f32[1024]{0:T(1024)S(1)} %bitcast.126, f32[4096]{0:T(1024)S(1)} %bitcast.116, f32[1024]{0:T(1024)S(1)} %bitcast.121, f32[4096]{0:T(1024)S(1)} %bitcast.101, ...), kind=kOutput, calls=%fused_computation.4 | convolution fusion | flops 1657143296 | bytes 737280 | tf_op jit(solution)/shard_map/dot_general | solution.py:51
  184.2 35.1 %all_to_all.98 = f32[8,32,1024]{2,1,0:T(8,128)S(1)} all-to-all(f32[8,32,1024]{2,1,0:T(8,128)S(1)} %broadcast_in_dim.66), channel_id=1, replica_groups=mesh['gx'=8,'gy'=16,'gz'=2] {'gx'}, dimensions={0} | all-to-all | bytes 2097152 | tf_op jit(solution)/shard_map/all_to_all | solution.py:19
  227.0 39.6 %all-gather.17.cloned.1.call-done = f32[1024,1024]{1,0:T(8,128)} async-done(((f32[32,1024]{1,0:T(8,128)}), f32[1024,1024]{1,0:T(8,128)}) %all-gather.17.cloned.1.call-update) | async-done | bytes 4194320 | tf_op jit(solution)/shard_map/all_gather | solution.py:14
  273.7 16.9 %fusion.2 = f32[32,1024]{1,0:T(8,128)S(1)} fusion(f32[1024]{0:T(1024)S(1)} %bitcast.132, f32[4096]{0:T(1024)S(1)} %bitcast.107, f32[1024]{0:T(1024)S(1)} %bitcast.137, f32[4096]{0:T(1024)S(1)} %bitcast.112, f32[1024]{0:T(1024)S(1)} %bitcast.127, f32[4096]{0:T(1024)S(1)} %bitcast.117, f32[1024]{0:T(1024)S(1)} %bitcast.122, f32[4096]{0:T(1024)S(1)} %bitcast.102, ...), kind=kOutput, calls=%fused_computation.3 | convolution fusion | flops 1657143296 | bytes 737280 | tf_op jit(solution)/shard_map/dot_general | solution.py:51
  291.7 6.7 %all-to-all-start.5 = ((f32[8,32,1024]{2,1,0:T(8,128)}), f32[8,32,1024]{2,1,0:T(8,128)S(1)}, u32[]{:S(2)}, u32[]{:S(2)}) async-start(f32[8,32,1024]{2,1,0:T(8,128)} %broadcast_in_dim.69), calls=%async_computation.5 | async-start | bytes 2097152 | tf_op jit(solution)/shard_map/all_to_all | solution.py:19
  298.5 29.1 %all-to-all-done.5 = f32[8,32,1024]{2,1,0:T(8,128)S(1)} async-done(((f32[8,32,1024]{2,1,0:T(8,128)}), f32[8,32,1024]{2,1,0:T(8,128)S(1)}, u32[]{:S(2)}, u32[]{:S(2)}) %all-to-all-start.5) | async-done | bytes 1048608 | tf_op jit(solution)/shard_map/all_to_all | solution.py:19
  328.7 14.3 %all_to_all.99 = f32[32,1,32]{2,1,0:T(1,128)S(1)} all-to-all(f32[32,1,32]{2,1,0:T(1,128)S(1)} %broadcast_in_dim.77), channel_id=1, replica_groups=mesh['gx'=8,'gy'=16,'gz'=2] {'gy','gz'}, dimensions={0} | all-to-all | bytes 8192 | tf_op jit(solution)/shard_map/all_to_all | solution.py:19
  343.0 10.7 %all_to_all.100 = f32[32,1,32]{2,1,0:T(1,128)S(1)} all-to-all(f32[32,1,32]{2,1,0:T(1,128)S(1)} %broadcast_in_dim.78), channel_id=1, replica_groups=mesh['gx'=8,'gy'=16,'gz'=2] {'gy','gz'}, dimensions={0} | all-to-all | bytes 8192 | tf_op jit(solution)/shard_map/all_to_all | solution.py:19
  358.4 18.0 %all-gather.19.cloned.1.call-done = f32[1024,1024]{1,0:T(8,128)} async-done(((f32[32,1024]{1,0:T(8,128)}), f32[1024,1024]{1,0:T(8,128)}) %all-gather.19.cloned.1.call-update) | async-done | bytes 4194320 | tf_op jit(solution)/shard_map/all_gather | solution.py:14
  383.4 16.6 %fusion.1 = f32[32,1024]{1,0:T(8,128)S(1)} fusion(f32[1024]{0:T(1024)S(1)} %bitcast.133, f32[4096]{0:T(1024)S(1)} %bitcast.108, f32[1024]{0:T(1024)S(1)} %bitcast.138, f32[4096]{0:T(1024)S(1)} %bitcast.113, f32[1024]{0:T(1024)S(1)} %bitcast.128, f32[4096]{0:T(1024)S(1)} %bitcast.118, f32[1024]{0:T(1024)S(1)} %bitcast.123, f32[4096]{0:T(1024)S(1)} %bitcast.103, ...), kind=kOutput, calls=%fused_computation.2 | convolution fusion | flops 1657143296 | bytes 737280 | tf_op jit(solution)/shard_map/dot_general | solution.py:51
  401.2 6.7 %all-to-all-start.8 = ((f32[8,32,1024]{2,1,0:T(8,128)}), f32[8,32,1024]{2,1,0:T(8,128)S(1)}, u32[]{:S(2)}, u32[]{:S(2)}) async-start(f32[8,32,1024]{2,1,0:T(8,128)} %broadcast_in_dim.72), calls=%async_computation.8 | async-start | bytes 2097152 | tf_op jit(solution)/shard_map/all_to_all | solution.py:19
  408.1 29.1 %all-to-all-done.8 = f32[8,32,1024]{2,1,0:T(8,128)S(1)} async-done(((f32[8,32,1024]{2,1,0:T(8,128)}), f32[8,32,1024]{2,1,0:T(8,128)S(1)}, u32[]{:S(2)}, u32[]{:S(2)}) %all-to-all-start.8) | async-done | bytes 1048608 | tf_op jit(solution)/shard_map/all_to_all | solution.py:19
  438.3 14.3 %all_to_all.101 = f32[32,1,32]{2,1,0:T(1,128)S(1)} all-to-all(f32[32,1,32]{2,1,0:T(1,128)S(1)} %broadcast_in_dim.79), channel_id=1, replica_groups=mesh['gx'=8,'gy'=16,'gz'=2] {'gy','gz'}, dimensions={0} | all-to-all | bytes 8192 | tf_op jit(solution)/shard_map/all_to_all | solution.py:19
  457.3 28.6 %all-gather.21.cloned.1.call-done = f32[1024,1024]{1,0:T(8,128)} async-done(((f32[32,1024]{1,0:T(8,128)}), f32[1024,1024]{1,0:T(8,128)}) %all-gather.21.cloned.1.call-update) | async-done | bytes 4194320 | tf_op jit(solution)/shard_map/all_gather | solution.py:14
  493.0 16.7 %fusion = f32[32,1024]{1,0:T(8,128)S(1)} fusion(f32[1024]{0:T(1024)S(1)} %bitcast.134, f32[4096]{0:T(1024)S(1)} %bitcast.109, f32[1024]{0:T(1024)S(1)} %bitcast.139, f32[4096]{0:T(1024)S(1)} %bitcast.114, f32[1024]{0:T(1024)S(1)} %bitcast.129, f32[4096]{0:T(1024)S(1)} %bitcast.119, f32[1024]{0:T(1024)S(1)} %bitcast.124, f32[4096]{0:T(1024)S(1)} %bitcast.104, ...), kind=kOutput, calls=%fused_computation.1 | convolution fusion | flops 1657143296 | bytes 737280 | tf_op jit(solution)/shard_map/dot_general | solution.py:51
  517.6 29.2 %all-to-all-done.11 = f32[8,32,1024]{2,1,0:T(8,128)S(1)} async-done(((f32[8,32,1024]{2,1,0:T(8,128)}), f32[8,32,1024]{2,1,0:T(8,128)S(1)}, u32[]{:S(2)}, u32[]{:S(2)}) %all-to-all-start.11) | async-done | bytes 1048608 | tf_op jit(solution)/shard_map/all_to_all | solution.py:19
  547.2 14.3 %all_to_all.102 = f32[32,1,32]{2,1,0:T(1,128)S(1)} all-to-all(f32[32,1,32]{2,1,0:T(1,128)S(1)} %broadcast_in_dim.76), channel_id=1, replica_groups=mesh['gx'=8,'gy'=16,'gz'=2] {'gy','gz'}, dimensions={0} | all-to-all | bytes 8192 | tf_op jit(solution)/shard_map/all_to_all | solution.py:19
  561.4 10.7 %all_to_all.103 = f32[32,1,32]{2,1,0:T(1,128)S(1)} all-to-all(f32[32,1,32]{2,1,0:T(1,128)S(1)} %broadcast_in_dim.74), channel_id=1, replica_groups=mesh['gx'=8,'gy'=16,'gz'=2] {'gy','gz'}, dimensions={0} | all-to-all | bytes 8192 | tf_op jit(solution)/shard_map/all_to_all | solution.py:19
  576.9 7.0 %all-to-all-done.16 = f32[32,1,32]{2,1,0:T(1,128)S(1)} async-done(((f32[32,1,32]{2,1,0:T(1,128)}), f32[32,1,32]{2,1,0:T(1,128)S(1)}, u32[]{:S(2)}, u32[]{:S(2)}) %all-to-all-start.16) | async-done | bytes 4128 | tf_op jit(solution)/shard_map/all_to_all | solution.py:19
  (92 shorter events, 62.5 us)
Async XLA Ops:
  7.2 58.7 %all-gather.13.cloned.1.call-start = ((), (), s32[]{:S(2)}) async-start(), calls=%async_computation.17 | async-start | bytes 4325376 | tf_op jit(solution)/shard_map/all_gather | solution.py:14
  7.9 158.4 %all-gather.15.cloned.1.call-start = ((), (), s32[]{:S(2)}) async-start(), calls=%async_computation.18 | async-start | bytes 4325376 | tf_op jit(solution)/shard_map/all_gather | solution.py:14
  83.9 35.3 %copy-start.3 = (f32[32,1024]{1,0:T(8,128)S(1)}, f32[32,1024]{1,0:T(8,128)}, u32[]{:S(2)}) copy-start(f32[32,1024]{1,0:T(8,128)} %param.7) | copy-start | bytes 393220
  83.9 35.3 %copy-start.5 = (f32[32,1024]{1,0:T(8,128)S(1)}, f32[32,1024]{1,0:T(8,128)}, u32[]{:S(2)}) copy-start(f32[32,1024]{1,0:T(8,128)} %param.6) | copy-start | bytes 393220
  84.0 35.3 %copy-start.6 = (f32[1024]{0:T(1024)S(1)}, f32[1024]{0:T(1024)}, u32[]{:S(2)}) copy-start(f32[1024]{0:T(1024)} %param.5) | copy-start | bytes 12292
  120.0 146.6 %all-gather.17.cloned.1.call-start = ((), (), s32[]{:S(2)}) async-start(), calls=%async_computation.19 | async-start | bytes 4325376 | tf_op jit(solution)/shard_map/all_gather | solution.py:14
  184.1 35.3 %copy-start = (f32[32,1024]{1,0:T(8,128)S(1)}, f32[32,1024]{1,0:T(8,128)}, u32[]{:S(2)}) copy-start(f32[32,1024]{1,0:T(8,128)} %add_subtract_fusion) | copy-start | bytes 393220
  220.9 46.8 %all-to-all-start.3 = ((f32[32,1,32]{2,1,0:T(1,128)}), f32[32,1,32]{2,1,0:T(1,128)S(1)}, u32[]{:S(2)}, u32[]{:S(2)}) async-start(f32[32,1,32]{2,1,0:T(1,128)} %broadcast_in_dim.67), calls=%async_computation.3 | async-start | bytes 32768 | tf_op jit(solution)/shard_map/all_to_all | solution.py:19
  268.4 22.2 %all-to-all-start.1 = ((f32[32,1,32]{2,1,0:T(1,128)}), f32[32,1,32]{2,1,0:T(1,128)S(1)}, u32[]{:S(2)}, u32[]{:S(2)}) async-start(f32[32,1,32]{2,1,0:T(1,128)} %broadcast_in_dim.65), calls=%async_computation.1 | async-start | bytes 32768 | tf_op jit(solution)/shard_map/all_to_all | solution.py:19
  290.5 37.2 %copy-start.1 = (f32[32,1024]{1,0:T(8,128)S(1)}, f32[32,1024]{1,0:T(8,128)}, u32[]{:S(2)}) copy-start(f32[32,1024]{1,0:T(8,128)} %get-tuple-element.30) | copy-start | bytes 393220
  291.7 36.0 %all-to-all-start.5 = ((f32[8,32,1024]{2,1,0:T(8,128)}), f32[8,32,1024]{2,1,0:T(8,128)S(1)}, u32[]{:S(2)}, u32[]{:S(2)}) async-start(f32[8,32,1024]{2,1,0:T(8,128)} %broadcast_in_dim.69), calls=%async_computation.5 | async-start | bytes 2097152 | tf_op jit(solution)/shard_map/all_to_all | solution.py:19
  298.4 78.0 %all-gather.19.cloned.1.call-start = ((), (), s32[]{:S(2)}) async-start(), calls=%async_computation.20 | async-start | bytes 4325376 | tf_op jit(solution)/shard_map/all_gather | solution.py:14
  354.3 23.2 %all-to-all-start.6 = ((f32[32,1,32]{2,1,0:T(1,128)}), f32[32,1,32]{2,1,0:T(1,128)S(1)}, u32[]{:S(2)}, u32[]{:S(2)}) async-start(f32[32,1,32]{2,1,0:T(1,128)} %broadcast_in_dim.70), calls=%async_computation.6 | async-start | bytes 32768 | tf_op jit(solution)/shard_map/all_to_all | solution.py:19
  378.1 22.0 %all-to-all-start.4 = ((f32[32,1,32]{2,1,0:T(1,128)}), f32[32,1,32]{2,1,0:T(1,128)S(1)}, u32[]{:S(2)}, u32[]{:S(2)}) async-start(f32[32,1,32]{2,1,0:T(1,128)} %broadcast_in_dim.68), calls=%async_computation.4 | async-start | bytes 32768 | tf_op jit(solution)/shard_map/all_to_all | solution.py:19
  400.1 37.2 %copy-start.2 = (f32[32,1024]{1,0:T(8,128)S(1)}, f32[32,1024]{1,0:T(8,128)}, u32[]{:S(2)}) copy-start(f32[32,1024]{1,0:T(8,128)} %get-tuple-element.28) | copy-start | bytes 393220
  401.2 36.0 %all-to-all-start.8 = ((f32[8,32,1024]{2,1,0:T(8,128)}), f32[8,32,1024]{2,1,0:T(8,128)S(1)}, u32[]{:S(2)}, u32[]{:S(2)}) async-start(f32[8,32,1024]{2,1,0:T(8,128)} %broadcast_in_dim.72), calls=%async_computation.8 | async-start | bytes 2097152 | tf_op jit(solution)/shard_map/all_to_all | solution.py:19
  408.0 78.0 %all-gather.21.cloned.1.call-start = ((), (), s32[]{:S(2)}) async-start(), calls=%async_computation.21 | async-start | bytes 4325376 | tf_op jit(solution)/shard_map/all_gather | solution.py:14
  453.1 33.9 %all-to-all-start.9 = ((f32[32,1,32]{2,1,0:T(1,128)}), f32[32,1,32]{2,1,0:T(1,128)S(1)}, u32[]{:S(2)}, u32[]{:S(2)}) async-start(f32[32,1,32]{2,1,0:T(1,128)} %broadcast_in_dim.73), calls=%async_computation.9 | async-start | bytes 32768 | tf_op jit(solution)/shard_map/all_to_all | solution.py:19
  487.7 22.0 %all-to-all-start.7 = ((f32[32,1,32]{2,1,0:T(1,128)}), f32[32,1,32]{2,1,0:T(1,128)S(1)}, u32[]{:S(2)}, u32[]{:S(2)}) async-start(f32[32,1,32]{2,1,0:T(1,128)} %broadcast_in_dim.71), calls=%async_computation.7 | async-start | bytes 32768 | tf_op jit(solution)/shard_map/all_to_all | solution.py:19
  509.7 37.2 %copy-start.4 = (f32[32,1024]{1,0:T(8,128)S(1)}, f32[32,1024]{1,0:T(8,128)}, u32[]{:S(2)}) copy-start(f32[32,1024]{1,0:T(8,128)} %get-tuple-element.22) | copy-start | bytes 393220
  510.8 36.0 %all-to-all-start.11 = ((f32[8,32,1024]{2,1,0:T(8,128)}), f32[8,32,1024]{2,1,0:T(8,128)S(1)}, u32[]{:S(2)}, u32[]{:S(2)}) async-start(f32[8,32,1024]{2,1,0:T(8,128)} %broadcast_in_dim.75), calls=%async_computation.11 | async-start | bytes 2097152 | tf_op jit(solution)/shard_map/all_to_all | solution.py:19
  572.7 11.2 %all-to-all-start.16 = ((f32[32,1,32]{2,1,0:T(1,128)}), f32[32,1,32]{2,1,0:T(1,128)S(1)}, u32[]{:S(2)}, u32[]{:S(2)}) async-start(f32[32,1,32]{2,1,0:T(1,128)} %broadcast_in_dim.80), calls=%async_computation.16 | async-start | bytes 32768 | tf_op jit(solution)/shard_map/all_to_all | solution.py:19
Sparse Core Ops, SparseCore 0:
  10.5 55.2 all-gather.12
  120.1 46.1 all-gather.14
  220.4 46.1 all-gather.16
  328.8 47.5 all-gather.18
  438.4 47.5 all-gather.20
where the time goes:
time: 602 us; the launch traced here: 592 us
  waiting for transfers between devices  258 us (43%)
  blocking collectives  161 us (27%)
  matrix products  83.8 us (14%)
  starting transfers between devices  54.9 us (9%)
  local copies, waits for them, and re-layouts  14.5 us (2%)
  between operations  14.4 us (2%)
    all_gather x5, waiting for transfers between devices, from_root(): lax.all_gather(shard, axis)  163 us
    all_to_all x7, blocking collectives, from_everyone(): return lax.all_to_all(copies, axis, split_axis=0, concat_axis=0, tiled=True)  134 us
    all_to_all x10, waiting for transfers between devices, from_everyone(): return lax.all_to_all(copies, axis, split_axis=0, concat_axis=0, tiled=True)  94.4 us
    dot_general x5, matrix products, matvec(): jnp.dot(row_part, kernel_block, precision=lax.Precision.HIGHEST)  83.8 us
    all_to_all x10, starting transfers between devices, from_everyone(): return lax.all_to_all(copies, axis, split_axis=0, concat_axis=0, tiled=True)  54.7 us
    all_gather x1, blocking collectives, from_root(): lax.all_gather(shard, axis)  26.4 us
  transfers between devices with their start and end apart: 15, of which 9 were waited for; matrix products, arithmetic and copies ran while one was open for 10% of the time, Pallas kernels for 0%

commit v1 on v0

v1 whole, which is shorter than its diff:
```python
import functools
import jax
import jax.numpy as jnp
from jax import lax
from jax.experimental import pallas as pl
from jax.experimental.pallas import tpu as pltpu
from jax.sharding import PartitionSpec as P

ITERS = 4
SOFT_SQ = 0.0025
LANE = 128
MESH = pl.DeviceIdType.MESH
F32 = jnp.float32
BF16 = jnp.bfloat16


def cg_kernel(np_, ngy, ngz, cases, chunk,
              panels, diagonal, right, start, sol_out, res_out, hist_out,
              rowpan, coords, ghi, glo, vp, vg, cz, ps, rs, acc, acc_lo,
              sol_c, r_c, s_c, d_c, r_r, s_r, zdir, gprev, aprev, hist, scal,
              dtile, dplane, dsum, dz,
              pan_s, pan_r, ag_s, ag_r, z_s, z_r, rs_s, rs_r, dp_s, dp_r, dz_s, dz_r):
    nq = ngy * ngz
    total = nq * np_ * LANE
    inv_root = total ** -0.5
    p = lax.axis_index("gx")
    gy = lax.axis_index("gy")
    gz = lax.axis_index("gz")
    q = gy * ngz + gz
    own = pl.ds(pl.multiple_of(p * LANE, LANE), LANE)
    span = 2 * LANE * chunk
    per_chunk = 2 * chunk
    lane = lax.broadcasted_iota(jnp.int32, (cases, LANE), 1)
    lane8 = lax.broadcasted_iota(jnp.int32, (8, LANE), 1)
    groups = cases // 8

    def plane_dev(k):
        other = lax.rem(q + k, nq)
        return other, (p, other // ngz, lax.rem(other, ngz))

    def z_dev(k):
        other = lax.rem(p + k, np_)
        return other, (other, gy, gz)

    def plane_copy(k, src, dst_of, send, recv_of):
        other, dev = plane_dev(k)
        out = pltpu.make_async_remote_copy(src, dst_of(q), send.at[k], recv_of(q), device_id=dev, device_id_type=MESH)
        inc = pltpu.make_async_remote_copy(src, dst_of(other), send.at[k], recv_of(other), device_id=dev, device_id_type=MESH)
        return out, inc

    def z_copy(k, src_of, dst_of, send, recv_of):
        other, dev = z_dev(k)
        out = pltpu.make_async_remote_copy(src_of(other), dst_of(p), send.at[k], recv_of(p), device_id=dev, device_id_type=MESH)
        inc = pltpu.make_async_remote_copy(src_of(other), dst_of(other), send.at[k], recv_of(other), device_id=dev, device_id_type=MESH)
        return out, inc

    def loop(lo, hi, fn):
        def step(i, carry):
            fn(i)
            return carry
        lax.fori_loop(lo, hi, step, 0)

    pan_copy = lambda k: plane_copy(k, panels.at[:, own], lambda s: rowpan.at[s], pan_s, lambda s: pan_r.at[s])
    ag_copy = lambda k, buf: plane_copy(k, vp, lambda s: vg.at[buf, s], ag_s, lambda s: ag_r.at[buf, s])
    zg_copy = lambda k, par: z_copy(k, lambda o: vp, lambda s: cz.at[par, s], z_s, lambda s: z_r.at[par, s])
    rs_copy = lambda k, par: z_copy(k, lambda o: ps.at[o], lambda s: rs.at[par, s], rs_s, lambda s: rs_r.at[par, s])
    dp_copy = lambda k: plane_copy(k, dtile, lambda s: dplane.at[s], dp_s, lambda s: dp_r.at[s])
    dz_copy = lambda k: z_copy(k, lambda o: dsum, lambda s: dz.at[s], dz_s, lambda s: dz_r.at[s])

    barrier = pltpu.get_barrier_semaphore()
    loop(1, nq, lambda k: pl.semaphore_signal(barrier, inc=1, device_id=plane_dev(k)[1], device_id_type=MESH))
    loop(1, np_, lambda k: pl.semaphore_signal(barrier, inc=1, device_id=z_dev(k)[1], device_id_type=MESH))
    vp[...] = start[:, own]
    pl.semaphore_wait(barrier, nq + np_ - 2)

    loop(1, nq, lambda k: pan_copy(k)[0].start())
    loop(1, nq, lambda k: ag_copy(k, 0)[0].start())
    rowpan[q] = panels[:, own]
    vg[0, q] = vp[...]
    ps[...] = jnp.zeros_like(ps)
    for s in range(np_):
        sol_c[s] = start[:, s * LANE:(s + 1) * LANE]
    s_c[...] = jnp.zeros_like(s_c)
    d_c[...] = jnp.zeros_like(d_c)
    r_c[...] = jnp.zeros_like(r_c)
    s_r[...] = jnp.zeros_like(s_r)
    r_r[...] = jnp.zeros_like(r_r)
    zdir[...] = jnp.zeros_like(zdir)
    gprev[...] = jnp.ones_like(gprev)
    aprev[...] = jnp.ones_like(aprev)
    hist[...] = jnp.zeros_like(hist)

    def build(slot):
        part = lax.div(slot, per_chunk)
        base = lax.rem(slot, per_chunk) * LANE
        for axis in range(3):
            coords[axis] = jnp.broadcast_to(rowpan[slot, axis:axis + 1, :], (LANE, LANE)).T
        rows_at = 32

        def block(i):
            here = pl.ds(pl.multiple_of(i * rows_at, rows_at), rows_at)
            there = pl.ds(pl.multiple_of(base + i * rows_at, rows_at), rows_at)
            x, y, z = coords[0, here, :], coords[1, here, :], coords[2, here, :]
            for ct in range(np_):
                cols = slice(ct * LANE, (ct + 1) * LANE)
                dx = x - panels[0:1, cols]
                dy = y - panels[1:2, cols]
                dzz = z - panels[2:3, cols]
                value = lax.rsqrt(dx * dx + dy * dy + dzz * dzz + SOFT_SQ)
                top = value.astype(BF16)
                ghi[part, there, cols] = top
                glo[part, there, cols] = (value - top.astype(F32)).astype(BF16)
        loop(0, LANE // rows_at, block)

    build(q)

    def build_other(k):
        pan_copy(k)[1].wait_recv()
        build(plane_dev(k)[0])
    loop(1, nq, build_other)
    loop(1, nq, lambda k: pan_copy(k)[0].wait_send())

    def pack_dots(sums):
        tile = jnp.zeros((8, LANE), F32)
        for d in range(3):
            for g in range(groups):
                tile = jnp.where(lane8 == groups * d + g, sums[d][8 * g:8 * g + 8, :], tile)
        return tile

    def unpack_dots(tile):
        out = []
        for d in range(3):
            out.append(jnp.concatenate([tile[:, groups * d + g:groups * d + g + 1] for g in range(groups)], 0))
        return out

    def row_sum(value):
        return jnp.sum(value, axis=1, keepdims=True)

    def coefficients(tile, turn):
        gamma, delta, omega = unpack_dots(tile)
        hist[...] = jnp.where(lane == turn, jnp.sqrt(omega / gamma), hist[...])
        gamma_prev = gprev[:, 0:1]
        alpha_prev = aprev[:, 0:1]
        beta = jnp.where(turn == 0, 0.0, gamma / gamma_prev)
        alpha = gamma / (delta - beta * gamma / alpha_prev)
        gprev[...] = jnp.broadcast_to(gamma, (cases, LANE))
        aprev[...] = jnp.broadcast_to(alpha, (cases, LANE))
        scal[...] = jnp.broadcast_to(beta, (cases, LANE))
        return alpha, beta

    def event(e, carry):
        par = lax.rem(e, 2)
        nxt = 1 - par
        turn = lax.rem(e, 3)
        after = lax.rem(e + 1, 3)
        loop(1, nq, lambda k: ag_copy(k, turn)[1].wait_recv())

        def matmul(c):
            pieces = []
            for i in range(per_chunk):
                slot = c * per_chunk + i
                value = vg[turn, slot] * (rowpan[slot, 3:4, :] * inv_root)
                top = value.astype(BF16)
                value = value - top.astype(F32)
                mid = value.astype(BF16)
                low = (value - mid.astype(F32)).astype(BF16)
                pieces.append(jnp.concatenate([top, mid, low], 0))
            lhs = jnp.concatenate(pieces, 1)
            main = jnp.dot(lhs, ghi[c], preferred_element_type=F32)
            rest = jnp.dot(lhs[:2 * cases], glo[c], preferred_element_type=F32)
            small = main[2 * cases:] + rest[cases:]
            acc[...] += main[:cases] + (main[cases:2 * cases] + rest[:cases] + small)

        acc[...] = jnp.zeros_like(acc)
        loop(0, nq // per_chunk, matmul)
        for s in range(np_):
            ps[s, 0:cases, :] = acc[:, s * LANE:(s + 1) * LANE]

        @pl.when(e >= 2)
        def _():
            def add(s, sums):
                r = r_r[s]
                a = vg[turn, s]
                return sums[0] + r * r, sums[1] + a * r, sums[2] + a * a
            zero = jnp.zeros((cases, LANE), F32)
            sums = lax.fori_loop(0, nq, add, (zero, zero, zero))
            tile = pack_dots([row_sum(v) for v in sums])
            for s in range(np_):
                ps[s, cases:, :] = tile

        loop(1, np_, lambda k: rs_copy(k, par)[0].start())
        rs[par, p] = ps[p]
        loop(1, nq, lambda k: ag_copy(k, turn)[0].wait_send())

        @pl.when(e > 0)
        def _():
            loop(1, np_, lambda k: zg_copy(k, par)[0].wait_send())
            cz[par, p] = vp[...]
        loop(1, np_, lambda k: rs_copy(k, par)[1].wait_recv())
        got = rs[par, 0]
        for s in range(1, np_):
            got = got + rs[par, s]
        fresh = got[:cases] * panels[3:4, own] + diagonal[0:1, own] * vp[...]

        @pl.when(e == 0)
        def _():
            vp[...] = right[:, own] - fresh

        @pl.when(e == 1)
        def _():
            vp[...] = fresh

        @pl.when(e >= 2)
        def _():
            alpha, beta = coefficients(got[cases:], e - 2)
            z = fresh + beta * zdir[...]
            zdir[...] = z
            vp[...] = vp[...] - alpha * z

        vg[after, q] = vp[...]

        @pl.when(e < ITERS)
        def _():
            loop(1, nq, lambda k: ag_copy(k, after)[0].start())
        loop(1, np_, lambda k: zg_copy(k, nxt)[0].start())
        loop(1, np_, lambda k: rs_copy(k, par)[0].wait_send())

        @pl.when(e > 0)
        def _():
            loop(1, np_, lambda k: zg_copy(k, par)[1].wait_recv())

        @pl.when(e == 1)
        def _():
            loop(0, nq, lambda s: r_r.__setitem__(s, vg[turn, s]))
            loop(0, np_, lambda s: r_c.__setitem__(s, cz[par, s]))

        @pl.when(e >= 2)
        def _():
            alpha = aprev[...]
            beta = scal[...]

            def rows(s):
                step = vg[turn, s] + beta * s_r[s]
                s_r[s] = step
                r_r[s] = r_r[s] - alpha * step
            loop(0, nq, rows)

            def cols(s):
                step = cz[par, s] + beta * s_c[s]
                s_c[s] = step
                along = r_c[s] + beta * d_c[s]
                d_c[s] = along
                sol_c[s] = sol_c[s] + alpha * along
                r_c[s] = r_c[s] - alpha * step
            loop(0, np_, cols)
        return carry

    lax.fori_loop(0, ITERS + 1, event, 0)

    last = (ITERS + 1) % 2
    r = r_c[p]
    a = vp[...]
    dtile[...] = pack_dots([row_sum(r * r), row_sum(a * r), row_sum(a * a)])
    loop(1, nq, lambda k: dp_copy(k)[0].start())
    dplane[q] = dtile[...]
    cz[last, p] = vp[...]
    loop(1, nq, lambda k: dp_copy(k)[1].wait_recv())
    dsum[...] = jnp.sum(dplane[...], axis=0)
    loop(1, np_, lambda k: dz_copy(k)[0].start())
    dz[p] = dsum[...]
    loop(1, nq, lambda k: dp_copy(k)[0].wait_send())
    loop(1, np_, lambda k: zg_copy(k, last)[0].wait_send())
    loop(1, np_, lambda k: zg_copy(k, last)[1].wait_recv())
    loop(1, np_, lambda k: dz_copy(k)[1].wait_recv())
    alpha, beta = coefficients(jnp.sum(dz[...], axis=0), ITERS - 1)
    for s in range(np_):
        cols = slice(s * LANE, (s + 1) * LANE)
        step = cz[last, s] + beta * s_c[s]
        along = r_c[s] + beta * d_c[s]
        sol_out[:, cols] = sol_c[s] + alpha * along
        res_out[:, cols] = r_c[s] - alpha * step
    hist_out[...] = hist[...].T[0:ITERS, :]
    loop(1, np_, lambda k: dz_copy(k)[0].wait_send())


def on_device(np_, ngy, ngz, panels, diagonal, right, start):
    nq = ngy * ngz
    cases, cols = right.shape
    chunk = min(4, nq // 2)
    span = 2 * LANE * chunk
    parts = nq // (2 * chunk)
    vm = lambda *shape: pltpu.VMEM(shape, F32)
    dma = lambda *shape: pltpu.SemaphoreType.DMA(shape)
    state = (np_, cases, LANE)
    wide = (nq, cases, LANE)
    one = (cases, LANE)
    scratch = [
        vm(nq, 4, LANE), vm(3, LANE, LANE),
        pltpu.VMEM((parts, span, cols), BF16), pltpu.VMEM((parts, span, cols), BF16),
        vm(*one), vm(3, *wide), vm(2, *state), vm(np_, cases + 8, LANE), vm(2, np_, cases + 8, LANE),
        vm(cases, cols), vm(8, LANE),
        vm(*state), vm(*state), vm(*state), vm(*state), vm(*wide), vm(*wide),
        vm(*one), vm(*one), vm(*one), vm(*one), vm(*one),
        vm(8, LANE), vm(nq, 8, LANE), vm(8, LANE), vm(np_, 8, LANE),
        dma(nq), dma(nq), dma(nq), dma(3, nq), dma(np_), dma(2, np_), dma(np_), dma(2, np_),
        dma(nq), dma(nq), dma(np_), dma(np_),
    ]
    return pl.pallas_call(
        functools.partial(cg_kernel, np_, ngy, ngz, cases, chunk),
        out_shape=(
            jax.ShapeDtypeStruct((cases, cols), F32),
            jax.ShapeDtypeStruct((cases, cols), F32),
            jax.ShapeDtypeStruct((ITERS, cases), F32),
        ),
        in_specs=[pl.BlockSpec(memory_space=pltpu.VMEM)] * 4,
        out_specs=tuple([pl.BlockSpec(memory_space=pltpu.VMEM)] * 3),
        scratch_shapes=scratch,
        compiler_params=pltpu.CompilerParams(
            collective_id=0, has_side_effects=True, vmem_limit_bytes=48 * 1024 * 1024
        ),
        name="cg",
    )(panels, diagonal[None, :], right, start)


def solution(mesh):
    cut = P(None, ("gy", "gz"))
    sizes = dict(mesh.shape)
    return jax.shard_map(
        functools.partial(on_device, sizes["gx"], sizes["gy"], sizes["gz"]),
        mesh=mesh,
        in_specs=(cut, P(("gy", "gz")), cut, cut),
        out_specs=(cut, cut, P()),
        check_vma=False,
    )
```

time: 602 us -> 137 us (0.23); the launches traced: 592 us -> 137 us
  waiting for transfers between devices: 258 us -> 0 us
  blocking collectives: 161 us -> 0 us
  Pallas kernels: 0 us -> 131 us
  matrix products: 83.8 us -> 0 us
  starting transfers between devices: 54.9 us -> 0 us
  between operations: 14.4 us -> 0.65 us
  local copies, waits for them, and re-layouts: 14.5 us -> 5.09 us
    all_gather x5 -> x0, waiting for transfers between devices: 163 us -> none  [from_root(): lax.all_gather(shard, axis)]
    all_to_all x7 -> x0, blocking collectives: 134 us -> none  [from_everyone(): return lax.all_to_all(copies, axis, split_axis=0, concat_axis=0, tiled=True)]
    pallas_call x0 -> x1, Pallas kernels: none -> 131 us  [on_device(): pl.pallas_call(functools.partial(cg_kernel, np_, ngy, ngz, cases, chunk),...]
    all_to_all x10 -> x0, waiting for transfers between devices: 94.4 us -> none  [from_everyone(): return lax.all_to_all(copies, axis, split_axis=0, concat_axis=0, tiled=True)]
    dot_general x5 -> x0, matrix products: 83.8 us -> none  [matvec(): jnp.dot(row_part, kernel_block, precision=lax.Precision.HIGHEST)]
    all_to_all x10 -> x0, starting transfers between devices: 54.7 us -> none  [from_everyone(): return lax.all_to_all(copies, axis, split_axis=0, concat_axis=0, tiled=True)]
    all_gather x1 -> x0, blocking collectives: 26.4 us -> none  [from_root(): lax.all_gather(shard, axis)]
    broadcast_in_dim x17 -> x0, local copies, waits for them, and re-layouts: 7.91 us -> none  [from_everyone(): copies = jnp.broadcast_to(shard, (lax.axis_size(axis), *shard.shape))]
  transfers between devices with their start and end apart: 15 -> 0, of which waited for: 9 -> 0; matrix products, arithmetic and copies ran while one was open for 10% -> 0% of each run, Pallas kernels for 0% -> 0%
where the time goes in v1:
time: 137 us
  Pallas kernels  131 us (96%)
  local copies, waits for them, and re-layouts  5.09 us (4%)
    pallas_call x1, Pallas kernels, on_device(): pl.pallas_call(functools.partial(cg_kernel, np_, ngy, ngz, cases, chunk),...  131 us
    unnamed x11, local copies, waits for them, and re-layouts  5.09 us

profile of v1, /device:TPU:1, one launch (start us, length us, event | category | flops | bytes accessed | tf_op | source)
XLA Modules:
  0.0 137.1 jit_solution(13753023980979431684)
XLA Ops:
  0.6 0.0 copy-start
  0.6 0.9 copy-done
  1.5 0.0 copy-start.1
  1.5 0.9 copy-done.1
  2.4 0.0 copy-start.2
  2.4 0.7 copy-done.2
  3.2 0.0 copy-start.3
  3.2 0.7 copy-done.3
  3.8 131.4 %cg.1 = (f32[32,1024]{1,0:T(8,128)S(1)}, f32[32,1024]{1,0:T(8,128)S(1)}, f32[4,32]{1,0:T(4,128)S(1)}) custom-call(f32[4,1024]{1,0:T(4,128)S(1)} %copy-done.2, f32[1,1024]{1,0:T(1,128)S(1)} %bitcast.1, f32[32,1024]{1,0:T(8,128)S(1)} %copy-done, f32[32,1024]{1,0:T(8,128)S(1)} %copy-done.1), custom_call_target="tpu_custom_call" | custom-call | tf_op jit(solution)/shard_map/cg/pallas_call | solution.py:308
  135.3 0.7 copy.10
  135.9 0.7 copy.11
  136.6 0.6 copy.12
Async XLA Ops:
  0.6 0.9 copy-start
  1.5 0.9 copy-start.1
  2.4 0.7 copy-start.2
  3.2 0.7 copy-start.3

commit v2 on v1

v2 whole, which is shorter than its diff:
```python
import functools
import math
import jax
import jax.numpy as jnp
from jax import lax
from jax.experimental import pallas as pl
from jax.experimental.pallas import tpu as pltpu
from jax.sharding import PartitionSpec as P

ITERS = 4
SOFT_SQ = 0.0025
LANE = 128
MESH = pl.DeviceIdType.MESH
F32 = jnp.float32
BF16 = jnp.bfloat16


def ring_distance(step, size):
    return min(step, size - step)


def chip_offsets(side):
    every = [(dx, dy) for dx in range(side) for dy in range(side)]
    return sorted(every, key=lambda o: (ring_distance(o[0], side) + ring_distance(o[1], side), o))


def send_order(side):
    hops = [ring_distance(dx, side) + ring_distance(dy, side) for dx, dy in chip_offsets(side)]
    near = [k for k in range(1, len(hops)) if hops[k] == 1]
    return near, list(range(len(hops) - 1, len(near), -1))


def arrival_order(side):
    near, rest = send_order(side)
    first = [(0, 0), (0, 1)]
    return first + [(k, c) for part in (near, rest) for c in range(2) for k in part]


def cg_kernel(np_, ngy, cases, per_chunk,
              panels_hbm, diagonal_hbm, right_hbm, start_hbm, sol_out, res_out, hist_out,
              panels, diagonal, right, start, rowpan, ghi, glo, rhs, lhs_last, vp, vg, cz, ps, rs, dots_out, dots_in, acc,
              sol_c, r_c, s_c, d_c, r_r, s_r, zdir, gprev, aprev, hist, scal, sums, dtile, dplane, dsum, dz,
              in_s, pan_s, pan_r, ag_s, ag_r, z_s, z_r, rs_s, rs_r, dt_s, dt_r, dp_s, dp_r, dz_s, dz_r):
    side = math.isqrt(ngy)
    offsets = chip_offsets(side)
    order = arrival_order(side)
    place = {slot: i for i, slot in enumerate(order)}
    nslot = len(order)
    nchunk = nslot // per_chunk
    inv_root = (nslot * np_ * LANE) ** -0.5
    p = lax.axis_index("gx")
    gy = lax.axis_index("gy")
    gz = lax.axis_index("gz")
    x, y = gy // side, lax.rem(gy, side)
    own = pl.ds(pl.multiple_of(p * LANE, LANE), LANE)
    lane = lax.broadcasted_iota(jnp.int32, (cases, LANE), 1)
    lane8 = lax.broadcasted_iota(jnp.int32, (8, LANE), 1)
    row8 = lax.broadcasted_iota(jnp.int32, (8, LANE), 0)
    groups = cases // 8
    far_z = sorted(range(1, np_), key=lambda d: -ring_distance(d, np_))
    near, rest = send_order(side)
    far_chip = near + rest

    def chip_at(k, sign):
        dx, dy = offsets[k]
        if sign < 0:
            dx, dy = (side - dx) % side, (side - dy) % side
        return lax.rem(x + dx, side) * side + lax.rem(y + dy, side)

    def chip(k, core):
        return (p, chip_at(k, -1), gz if core == 0 else 1 - gz)

    def z_of(d):
        return lax.rem(p + d, np_)

    def z_dev(d):
        return (z_of(d), gy, gz)

    def remote(src, dst, send, recv, dev):
        return pltpu.make_async_remote_copy(src, dst, send, recv, device_id=dev, device_id_type=MESH)

    def loop(lo, hi, fn):
        def step(i, carry):
            fn(i)
            return carry
        lax.fori_loop(lo, hi, step, 0)

    def everyone_copy(k, core, src, dst, send, recv):
        i = place[k, core]
        return remote(src, dst.at[i], send.at[i], recv.at[i], chip(k, core))

    peers = [s for s in order if s != (0, 0)]

    def ag_copy(k, core, buf):
        i = place[k, core]
        return remote(vp, vg.at[buf, i], ag_s.at[i], ag_r.at[buf, i], chip(k, core))

    def relay_copy(k, buf):
        i, j = place[k, 0], place[k, 1]
        return remote(vg.at[buf, i], vg.at[buf, j], ag_s.at[j], ag_r.at[buf, j], (p, gy, 1 - gz))

    def zg_send(d, par):
        return remote(vp, cz.at[par, p], z_s.at[d], z_r.at[par, p], z_dev(d))

    def zg_recv(d, par):
        o = z_of(d)
        return remote(vp, cz.at[par, o], z_s.at[d], z_r.at[par, o], z_dev(d))

    def rs_copy(d, par):
        return remote(ps.at[z_of(d)], rs.at[par, d], rs_s.at[d], rs_r.at[par, d], z_dev(d))

    def dt_copy(d, par):
        return remote(dots_out, dots_in.at[par, d], dt_s.at[d], dt_r.at[par, d], z_dev(d))

    def dz_copy(d):
        return remote(dsum, dz.at[d], dz_s.at[d], dz_r.at[d], z_dev(d))

    loads = [
        pltpu.make_async_copy(panels_hbm, panels, in_s.at[0]),
        pltpu.make_async_copy(start_hbm.at[:, own], vp, in_s.at[1]),
        pltpu.make_async_copy(start_hbm, start, in_s.at[2]),
        pltpu.make_async_copy(right_hbm, right, in_s.at[3]),
        pltpu.make_async_copy(diagonal_hbm, diagonal, in_s.at[4]),
    ]
    for load in loads:
        load.start()

    barrier = pltpu.get_barrier_semaphore()
    for k, core in reversed(peers):
        pl.semaphore_signal(barrier, inc=1, device_id=chip(k, core), device_id_type=MESH)
    for d in far_z:
        pl.semaphore_signal(barrier, inc=1, device_id=z_dev(d), device_id_type=MESH)

    loads[0].wait()
    rowpan[0] = panels[:, own]

    def split(value):
        top = value.astype(BF16).astype(F32)
        mid = (value - top).astype(BF16).astype(F32)
        return top, mid, value - top - mid

    row_n = lax.broadcasted_iota(jnp.int32, (8, LANE), 0)
    for s in range(np_):
        cols = slice(s * LANE, (s + 1) * LANE)
        ax, ay, at = (panels[i:i + 1, cols] for i in range(3))
        other = jnp.where(row_n == 4, 1.0, jnp.where(row_n == 5, ax * ax + ay * ay + at * at, 0.0))
        for i, value in enumerate((ax, ay, at)):
            other = jnp.where(row_n == i, -2.0 * value, other)
        top, mid, low = split(other)
        rhs[:, cols] = jnp.concatenate([top, mid, low, top, mid, top], 0).astype(BF16)

    for load in loads[1:]:
        load.wait()
    vg[0, 0] = vp[...]
    for s in range(np_):
        sol_c[s] = start[:, s * LANE:(s + 1) * LANE]
    dots_out[...] = jnp.zeros_like(dots_out)
    s_c[...] = jnp.zeros_like(s_c)
    d_c[...] = jnp.zeros_like(d_c)
    r_c[...] = jnp.zeros_like(r_c)
    s_r[...] = jnp.zeros_like(s_r)
    r_r[...] = jnp.zeros_like(r_r)
    zdir[...] = jnp.zeros_like(zdir)
    gprev[...] = jnp.ones_like(gprev)
    aprev[...] = jnp.ones_like(aprev)
    hist[...] = jnp.zeros_like(hist)

    with jax.named_scope("barrier"):
        pl.semaphore_wait(barrier, nslot - 1 + np_ - 1)
    def pan_copy(k, core):
        return everyone_copy(k, core, panels.at[:, own], rowpan, pan_s, pan_r)

    for k, core in sorted(peers, key=lambda s: -s[0]):
        pan_copy(k, core).start()

    def send_piece(buf):
        for k in far_chip:
            ag_copy(k, 0, buf).start()
        ag_copy(0, 1, buf).start()

    send_piece(0)

    def build(c):
        for n, (k, core) in enumerate(order[c * per_chunk:(c + 1) * per_chunk]):
            i = c * per_chunk + n
            pan = rowpan[i]
            ax, ay, at = (pan[j:j + 1] for j in range(3))
            tile = jnp.where(row8 == 4, ax * ax + ay * ay + at * at + SOFT_SQ, jnp.where(row8 == 5, 1.0, 0.0))
            for j, value in enumerate((ax, ay, at)):
                tile = jnp.where(row8 == j, value, tile)
            top, mid, low = split(tile)
            lhs = jnp.concatenate([top, top, top, mid, mid, low], 0).T.astype(BF16)
            there = slice(n * LANE, (n + 1) * LANE)
            for t in range(np_ * LANE // width):
                cols = slice(t * width, (t + 1) * width)
                value = lax.rsqrt(jnp.dot(lhs, rhs[:, cols], preferred_element_type=F32))
                top = value.astype(BF16)
                ghi[c, there, cols] = top
                glo[c, there, cols] = (value - top.astype(F32)).astype(BF16)

    width = 2 * LANE

    def pack_dots(parts):
        out = jnp.zeros((8, LANE), F32)
        for d in range(3):
            for g in range(groups):
                out = jnp.where(lane8 == groups * d + g, parts[d][8 * g:8 * g + 8, :], out)
        return out

    def unpack_dots(got):
        out = []
        for d in range(3):
            out.append(jnp.concatenate([got[:, groups * d + g:groups * d + g + 1] for g in range(groups)], 0))
        return out

    def row_sum(value):
        return jnp.sum(value, axis=1, keepdims=True)

    def coefficients(got, turn):
        gamma, delta, omega = unpack_dots(got)
        hist[...] = jnp.where(lane == turn, jnp.sqrt(omega / gamma), hist[...])
        gamma_prev = gprev[:, 0:1]
        alpha_prev = aprev[:, 0:1]
        beta = jnp.where(turn == 0, 0.0, gamma / gamma_prev)
        alpha = gamma / (delta - beta * gamma / alpha_prev)
        gprev[...] = jnp.broadcast_to(gamma, (cases, LANE))
        aprev[...] = jnp.broadcast_to(alpha, (cases, LANE))
        scal[...] = jnp.broadcast_to(beta, (cases, LANE))
        return alpha, beta

    def rows_of(c, buf):
        pieces = []
        for i in range(c * per_chunk, (c + 1) * per_chunk):
            value = vg[buf, i] * (rowpan[i, 3:4, :] * inv_root)
            top = value.astype(BF16)
            value = value - top.astype(F32)
            mid = value.astype(BF16)
            low = (value - mid.astype(F32)).astype(BF16)
            pieces.append(jnp.concatenate([top, mid, low], 0))
        return jnp.concatenate(pieces, 1)

    def product(lhs, top, low):
        main = jnp.dot(lhs, top, preferred_element_type=F32)
        rest = jnp.dot(lhs[:2 * cases], low, preferred_element_type=F32)
        small = main[2 * cases:] + rest[cases:]
        return main[:cases] + (main[cases:2 * cases] + rest[:cases] + small)

    def matmul(c, buf):
        part = product(rows_of(c, buf), ghi[c], glo[c])
        acc[...] = part if c == 0 else part + acc[...]

    def last_matmul(buf, par):
        c = nchunk - 1
        lhs_last[...] = rows_of(c, buf)
        half = np_ // 2
        for turn in (1, 0):
            j = lax.rem(lax.div(p, half) + turn, 2)
            cols = pl.ds(pl.multiple_of(j * (half * LANE), half * LANE), half * LANE)
            part = acc[:, cols] + product(lhs_last[...], ghi[c, :, cols], glo[c, :, cols])
            for h in range(half):
                ps[half * j + h] = part[:, h * LANE:(h + 1) * LANE]
            for h in range(half):
                to = half * j + h
                d = lax.rem(to + np_ - p, np_)

                @pl.when(d > 0)
                def _():
                    remote(ps.at[to], rs.at[par, d], rs_s.at[d], rs_r.at[par, d], (to, gy, gz)).start()

    def dots(first, stop, buf, parts):
        g, d, o = parts
        for i in range(first, stop):
            r, a = r_r[i], vg[buf, i]
            g, d, o = g + r * r, d + a * r, o + a * a
        return g, d, o

    def arrive(c, buf):
        with jax.named_scope(f"ag_wait{c}"):
            need = order[c * per_chunk:(c + 1) * per_chunk]
            direct = [k for k, core in need if core == 0 and k > 0]
            if c == 1:
                direct = [k for k in far_chip if place[k, 0] >= per_chunk]
            elif c > 1:
                direct = []
            for k in direct:
                ag_copy(k, 0, buf).wait_recv()
                relay_copy(k, buf).start()
            for k, core in need:
                if core == 1:
                    ag_copy(k, 1, buf).wait_recv()

    with jax.named_scope("build"):
        for c in range(nchunk):
            with jax.named_scope(f"pan_wait{c}"):
                for k, core in order[c * per_chunk:(c + 1) * per_chunk]:
                    if (k, core) != (0, 0):
                        pan_copy(k, core).wait_recv()
            if c > 0:
                arrive(c - 1, 0)
            build(c)
            if c > 0:
                matmul(c - 1, 0)
        arrive(nchunk - 1, 0)
    for k, core in peers:
        pan_copy(k, core).wait_send()

    def event(e, carry):
        par = lax.rem(e, 2)
        nxt = 1 - par
        buf = lax.rem(e, 3)
        after = lax.rem(e + 1, 3)
        @pl.when(e > 0)
        def _():
            for c in range(nchunk - 1):
                arrive(c, buf)
                if c == nchunk - 2:
                    arrive(c + 1, buf)
                with jax.named_scope(f"matmul{c}"):
                    matmul(c, buf)
                    parts = (sums[0], sums[1], sums[2])
                    if c == 0:
                        parts = (jnp.zeros((cases, LANE), F32),) * 3
                    stop = (c + 1) * per_chunk if c < nchunk - 2 else nslot
                    parts = dots(c * per_chunk, stop, buf, parts)
                    if c < nchunk - 2:
                        sums[0], sums[1], sums[2] = parts
                    else:
                        dots_out[...] = pack_dots([row_sum(v) for v in parts])
            for d in far_z:
                dt_copy(d, par).start()
        with jax.named_scope("matmul3"):
            last_matmul(buf, par)
        dots_in[par, 0] = dots_out[...]
        rs[par, 0] = ps[p]
        for k in far_chip:
            ag_copy(k, 0, buf).wait_send()
            relay_copy(k, buf).wait_send()
        ag_copy(0, 1, buf).wait_send()

        @pl.when(e > 0)
        def _():
            for d in far_z:
                zg_send(d, par).wait_send()
            cz[par, p] = vp[...]
        with jax.named_scope("rs_wait"):
            @pl.when(e > 0)
            def _():
                for d in far_z:
                    dt_copy(d, par).wait_recv()
            for d in far_z:
                rs_copy(d, par).wait_recv()
        got = jnp.sum(rs[par], axis=0)
        fresh = got * panels[3:4, own] + diagonal[0:1, own] * vp[...]

        @pl.when(e == 0)
        def _():
            vp[...] = right[:, own] - fresh

        @pl.when(e == 1)
        def _():
            vp[...] = fresh

        @pl.when(e >= 2)
        def _():
            alpha, beta = coefficients(jnp.sum(dots_in[par], axis=0), e - 2)
            z = fresh + beta * zdir[...]
            zdir[...] = z
            vp[...] = vp[...] - alpha * z

        @pl.when(e < ITERS)
        def _():
            send_piece(after)
        for d in far_z:
            zg_send(d, nxt).start()
        vg[after, 0] = vp[...]
        with jax.named_scope("rs_send"):
            for d in far_z:
                rs_copy(d, par).wait_send()

        @pl.when(e > 0)
        def _():
            for d in far_z:
                dt_copy(d, par).wait_send()
            for d in far_z:
                zg_recv(d, par).wait_recv()

        @pl.when(e == 1)
        def _():
            loop(0, nslot, lambda s: r_r.__setitem__(s, vg[buf, s]))
            loop(0, np_, lambda s: r_c.__setitem__(s, cz[par, s]))

        @pl.when(e >= 2)
        def _():
            alpha = aprev[...]
            beta = scal[...]

            def rows(s):
                step = vg[buf, s] + beta * s_r[s]
                s_r[s] = step
                r_r[s] = r_r[s] - alpha * step
            loop(0, nslot, rows)

            def cols(s):
                step = cz[par, s] + beta * s_c[s]
                s_c[s] = step
                along = r_c[s] + beta * d_c[s]
                d_c[s] = along
                sol_c[s] = sol_c[s] + alpha * along
                r_c[s] = r_c[s] - alpha * step
            loop(0, np_, cols)
        return carry

    lax.fori_loop(0, ITERS + 1, event, 0)

    last = (ITERS + 1) % 2
    r = r_c[p]
    a = vp[...]
    dtile[...] = pack_dots([row_sum(r * r), row_sum(a * r), row_sum(a * a)])
    for k, core in reversed(peers):
        everyone_copy(k, core, dtile, dplane, dp_s, dp_r).start()
    dplane[0] = dtile[...]
    cz[last, p] = vp[...]
    with jax.named_scope("dp_wait"):
        for k, core in peers:
            everyone_copy(k, core, dtile, dplane, dp_s, dp_r).wait_recv()
    dsum[...] = jnp.sum(dplane[...], axis=0)
    for d in far_z:
        dz_copy(d).start()
    dz[0] = dsum[...]
    for k, core in peers:
        everyone_copy(k, core, dtile, dplane, dp_s, dp_r).wait_send()
    for d in far_z:
        zg_send(d, last).wait_send()
    with jax.named_scope("dz_wait"):
        for d in far_z:
            zg_recv(d, last).wait_recv()
        for d in far_z:
            dz_copy(d).wait_recv()
    alpha, beta = coefficients(jnp.sum(dz[...], axis=0), ITERS - 1)
    for s in range(np_):
        cols = slice(s * LANE, (s + 1) * LANE)
        step = cz[last, s] + beta * s_c[s]
        along = r_c[s] + beta * d_c[s]
        sol_out[:, cols] = sol_c[s] + alpha * along
        res_out[:, cols] = r_c[s] - alpha * step
    hist_out[...] = hist[...].T[0:ITERS, :]
    for d in far_z:
        dz_copy(d).wait_send()


def on_device(np_, ngy, panels, diagonal, right, start):
    cases, cols = right.shape
    nslot = 2 * ngy
    per_chunk = nslot // 4
    span = LANE * per_chunk
    parts = nslot // per_chunk
    vm = lambda *shape: pltpu.VMEM(shape, F32)
    dma = lambda *shape: pltpu.SemaphoreType.DMA(shape)
    state = (np_, cases, LANE)
    wide = (nslot, cases, LANE)
    one = (cases, LANE)
    scratch = [
        vm(4, cols), vm(1, cols), vm(cases, cols), vm(cases, cols),
        vm(nslot, 4, LANE),
        pltpu.VMEM((parts, span, cols), BF16), pltpu.VMEM((parts, span, cols), BF16), pltpu.VMEM((48, cols), BF16), pltpu.VMEM((3 * cases, span), BF16),
        vm(*one), vm(3, *wide), vm(2, *state), vm(np_, *one), vm(2, np_, *one), vm(8, LANE), vm(2, np_, 8, LANE),
        vm(cases, cols),
        vm(*state), vm(*state), vm(*state), vm(*state), vm(*wide), vm(*wide),
        vm(*one), vm(*one), vm(*one), vm(*one), vm(*one), vm(3, *one),
        vm(8, LANE), vm(nslot, 8, LANE), vm(8, LANE), vm(np_, 8, LANE),
        dma(5), dma(nslot), dma(nslot), dma(nslot), dma(3, nslot), dma(np_), dma(2, np_), dma(np_), dma(2, np_), dma(np_), dma(2, np_),
        dma(nslot), dma(nslot), dma(np_), dma(np_),
    ]
    return pl.pallas_call(
        functools.partial(cg_kernel, np_, ngy, cases, per_chunk),
        out_shape=(
            jax.ShapeDtypeStruct((cases, cols), F32),
            jax.ShapeDtypeStruct((cases, cols), F32),
            jax.ShapeDtypeStruct((ITERS, cases), F32),
        ),
        in_specs=[pl.BlockSpec(memory_space=pltpu.HBM)] * 4,
        out_specs=tuple([pl.BlockSpec(memory_space=pltpu.VMEM)] * 3),
        scratch_shapes=scratch,
        compiler_params=pltpu.CompilerParams(
            collective_id=0, has_side_effects=True, vmem_limit_bytes=60 * 1024 * 1024
        ),
        name="cg",
    )(panels, diagonal[None, :], right, start)


def solution(mesh):
    cut = P(None, ("gy", "gz"))
    sizes = dict(mesh.shape)
    return jax.shard_map(
        functools.partial(on_device, sizes["gx"], sizes["gy"]),
        mesh=mesh,
        in_specs=(cut, P(("gy", "gz")), cut, cut),
        out_specs=(cut, cut, P()),
        check_vma=False,
    )
```

time: 137 us -> 106 us (0.77)
  Pallas kernels: 131 us -> 102 us
  local copies, waits for them, and re-layouts: 5.09 us -> 2.86 us
    pallas_call x1, Pallas kernels: 131 us -> 102 us  [on_device(): pl.pallas_call(functools.partial(cg_kernel, np_, ngy, cases, per_chunk),...]
    unnamed x11 -> x7, local copies, waits for them, and re-layouts: 5.09 us -> 2.86 us
where the time goes in v2:
time: 106 us
  Pallas kernels  102 us (96%)
  local copies, waits for them, and re-layouts  2.86 us (3%)
    pallas_call x1, Pallas kernels, on_device(): pl.pallas_call(functools.partial(cg_kernel, np_, ngy, cases, per_chunk),...  102 us
    unnamed x7, local copies, waits for them, and re-layouts  2.86 us

profile of v2, /device:TPU:1, one launch (start us, length us, event | category | flops | bytes accessed | tf_op | source)
XLA Modules:
  0.0 105.7 jit_solution(14449706625009308715)
XLA Ops:
  0.6 102.2 %cg.1 = (f32[32,1024]{1,0:T(8,128)}, f32[32,1024]{1,0:T(8,128)}, f32[4,32]{1,0:T(4,128)}) custom-call(f32[4,1024]{1,0:T(4,128)} %panels_hbm.1, f32[1,1024]{1,0:T(1,128)} %bitcast.1, f32[32,1024]{1,0:T(8,128)} %right_hbm.1, f32[32,1024]{1,0:T(8,128)} %start_hbm.1), custom_call_target="tpu_custom_call" | custom-call | tf_op jit(solution)/shard_map/cg/pallas_call | solution.py:474
  102.8 0.0 copy-start
  102.8 1.6 %copy.10 = f32[32,1024]{1,0:T(8,128)} copy(f32[32,1024]{1,0:T(8,128)} %get-tuple-element.6) | data formatting | bytes 262144
  104.4 0.0 copy-done
  104.4 0.0 copy-start.1
  104.4 0.7 copy.11
  105.1 0.0 copy-done.1
  105.1 0.6 copy.12
Async XLA Ops:
  102.8 1.6 %copy-start = (f32[32,1024]{1,0:T(8,128)S(1)}, f32[32,1024]{1,0:T(8,128)}, u32[]{:S(2)}) copy-start(f32[32,1024]{1,0:T(8,128)} %get-tuple-element.7) | copy-start | bytes 393220
  104.4 0.7 copy-start.1

commit v3 on v2

v3 whole, which is shorter than its diff:
```python
import functools
import math
import jax
import jax.numpy as jnp
from jax import lax
from jax.experimental import pallas as pl
from jax.experimental.pallas import tpu as pltpu
from jax.sharding import PartitionSpec as P

ITERS = 4
SOFT_SQ = 0.0025
LANE = 128
MESH = pl.DeviceIdType.MESH
F32 = jnp.float32
BF16 = jnp.bfloat16


def ring_distance(step, size):
    return min(step, size - step)


def chip_offsets(side):
    every = [(dx, dy) for dx in range(side) for dy in range(side)]
    return sorted(every, key=lambda o: (ring_distance(o[0], side) + ring_distance(o[1], side), o))


def cg_kernel(np_, ngy, cases, per_chunk,
              panels_hbm, diagonal_hbm, right_hbm, start_hbm, sol_out, res_out, hist_out,
              panels, partner, diagonal, right, start, rowpan, ghi, glo, rhs, lhs_last, vp, vg, cz, px, px_in, ps, rs,
              dots_out, dots_in, acc, sol_c, r_c, s_c, d_c, r_r, s_r, zdir, gprev, aprev, hist, scal, sums,
              dtile, dplane, dsum, dz,
              in_s, pan_s, pan_r, pp_s, pp_r, ag_s, ag_r, z_s, z_r, px_s, px_r, rs_s, rs_r, dt_s, dt_r,
              dp_s, dp_r, dz_s, dz_r):
    side = math.isqrt(ngy)
    offsets = chip_offsets(side)
    order = list(range(ngy))
    place = {k: i for i, k in enumerate(order)}
    nslot = len(order)
    nchunk = nslot // per_chunk
    cols_all = np_ * LANE
    inv_root = (2 * nslot * np_ * LANE) ** -0.5
    p = lax.axis_index("gx")
    gy = lax.axis_index("gy")
    gz = lax.axis_index("gz")
    x, y = gy // side, lax.rem(gy, side)
    own = pl.ds(pl.multiple_of(p * LANE, LANE), LANE)
    lane = lax.broadcasted_iota(jnp.int32, (cases, LANE), 1)
    lane8 = lax.broadcasted_iota(jnp.int32, (8, LANE), 1)
    row8 = lax.broadcasted_iota(jnp.int32, (8, LANE), 0)
    groups = cases // 8
    far_z = sorted(range(1, np_), key=lambda d: -ring_distance(d, np_))
    every_chip = range(ngy)
    everyone = [(k, core) for k in range(ngy) for core in range(2) if k + core]

    def chip_at(k, sign):
        dx, dy = offsets[k]
        if sign < 0:
            dx, dy = (side - dx) % side, (side - dy) % side
        return lax.rem(x + dx, side) * side + lax.rem(y + dy, side)

    def chip(k, core):
        return (p, chip_at(k, -1), gz if core == 0 else 1 - gz)

    def z_of(d):
        return lax.rem(p + d, np_)

    def z_dev(d):
        return (z_of(d), gy, gz)

    def remote(src, dst, send, recv, dev):
        return pltpu.make_async_remote_copy(src, dst, send, recv, device_id=dev, device_id_type=MESH)

    def loop(lo, hi, fn):
        def step(i, carry):
            fn(i)
            return carry
        lax.fori_loop(lo, hi, step, 0)

    def plane_copy(k, core):
        i = 2 * k + core
        return remote(dtile, dplane.at[i], dp_s.at[i], dp_r.at[i], chip(k, core))

    def pan_copy(k):
        i = place[k]
        return remote(panels.at[:, own], rowpan.at[i], pan_s.at[i], pan_r.at[i], chip(k, 1))

    def partner_copy():
        return remote(panels, partner, pp_s, pp_r, chip(0, 1))

    def ag_copy(k, buf):
        i = place[k]
        return remote(vp, vg.at[buf, i], ag_s.at[i], ag_r.at[buf, i], chip(k, 1))

    def px_copy(par):
        return remote(px, px_in.at[par], px_s, px_r.at[par], chip(0, 1))

    def zg_send(d, par):
        return remote(vp, cz.at[par, p], z_s.at[d], z_r.at[par, p], z_dev(d))

    def zg_recv(d, par):
        o = z_of(d)
        return remote(vp, cz.at[par, o], z_s.at[d], z_r.at[par, o], z_dev(d))

    def rs_copy(d, par):
        return remote(ps.at[z_of(d)], rs.at[par, d], rs_s.at[d], rs_r.at[par, d], (z_of(d), gy, 1 - gz))

    def dt_copy(d, core, par):
        i = 2 * d + core
        return remote(dots_out, dots_in.at[par, i], dt_s.at[i], dt_r.at[par, i], (z_of(d), gy, gz if core == 0 else 1 - gz))

    dot_peers = [(d, core) for d in far_z + [0] for core in range(2) if d + core]

    def dz_copy(d):
        return remote(dsum, dz.at[d], dz_s.at[d], dz_r.at[d], (z_of(d), gy, 1 - gz))

    loads = [
        pltpu.make_async_copy(panels_hbm, panels, in_s.at[0]),
        pltpu.make_async_copy(start_hbm.at[:, own], vp, in_s.at[1]),
        pltpu.make_async_copy(start_hbm, start, in_s.at[2]),
        pltpu.make_async_copy(right_hbm, right, in_s.at[3]),
        pltpu.make_async_copy(diagonal_hbm, diagonal, in_s.at[4]),
    ]
    for load in loads:
        load.start()

    barrier = pltpu.get_barrier_semaphore()
    for k, core in reversed(everyone):
        pl.semaphore_signal(barrier, inc=1, device_id=chip(k, core), device_id_type=MESH)
    for d in far_z:
        for core in range(2):
            dev = (z_of(d), gy, gz if core == 0 else 1 - gz)
            pl.semaphore_signal(barrier, inc=1, device_id=dev, device_id_type=MESH)

    loads[0].wait()

    def split(value):
        top = value.astype(BF16).astype(F32)
        mid = (value - top).astype(BF16).astype(F32)
        return top, mid, value - top - mid

    def other_side(pan, base):
        for s in range(np_):
            here = slice(s * LANE, (s + 1) * LANE)
            ax, ay, at = (pan[i:i + 1, here] for i in range(3))
            other = jnp.where(row8 == 4, 1.0, jnp.where(row8 == 5, ax * ax + ay * ay + at * at, 0.0))
            for i, value in enumerate((ax, ay, at)):
                other = jnp.where(row8 == i, -2.0 * value, other)
            top, mid, low = split(other)
            there = slice(base + s * LANE, base + (s + 1) * LANE)
            rhs[:, there] = jnp.concatenate([top, mid, low, top, mid, top], 0).astype(BF16)

    other_side(panels, 0)

    for load in loads[1:]:
        load.wait()
    for s in range(np_):
        sol_c[s] = start[:, s * LANE:(s + 1) * LANE]
    sums[...] = jnp.zeros_like(sums)
    s_c[...] = jnp.zeros_like(s_c)
    d_c[...] = jnp.zeros_like(d_c)
    r_c[...] = jnp.zeros_like(r_c)
    s_r[...] = jnp.zeros_like(s_r)
    r_r[...] = jnp.zeros_like(r_r)
    zdir[...] = jnp.zeros_like(zdir)
    gprev[...] = jnp.ones_like(gprev)
    aprev[...] = jnp.ones_like(aprev)
    hist[...] = jnp.zeros_like(hist)

    with jax.named_scope("barrier"):
        pl.semaphore_wait(barrier, 2 * ngy - 1 + 2 * (np_ - 1))
    partner_copy().start()
    for k in reversed(every_chip):
        pan_copy(k).start()

    def send_piece(buf):
        for k in every_chip:
            ag_copy(k, buf).start()

    send_piece(0)
    partner_copy().wait_recv()
    other_side(partner, cols_all)

    def build(c):
        for n in range(per_chunk):
            i = c * per_chunk + n
            pan = rowpan[i]
            ax, ay, at = (pan[j:j + 1] for j in range(3))
            tile = jnp.where(row8 == 4, ax * ax + ay * ay + at * at + SOFT_SQ, jnp.where(row8 == 5, 1.0, 0.0))
            for j, value in enumerate((ax, ay, at)):
                tile = jnp.where(row8 == j, value, tile)
            top, mid, low = split(tile)
            lhs = jnp.concatenate([top, top, top, mid, mid, low], 0).T.astype(BF16)
            there = slice(n * LANE, (n + 1) * LANE)
            for t in range(2 * cols_all // width):
                cols = slice(t * width, (t + 1) * width)
                value = lax.rsqrt(jnp.dot(lhs, rhs[:, cols], preferred_element_type=F32))
                top = value.astype(BF16)
                ghi[c, there, cols] = top
                glo[c, there, cols] = (value - top.astype(F32)).astype(BF16)

    width = 2 * LANE

    def pack_dots(parts):
        out = jnp.zeros((8, LANE), F32)
        for d in range(3):
            for g in range(groups):
                out = jnp.where(lane8 == groups * d + g, parts[d][8 * g:8 * g + 8, :], out)
        return out

    def unpack_dots(got):
        out = []
        for d in range(3):
            out.append(jnp.concatenate([got[:, groups * d + g:groups * d + g + 1] for g in range(groups)], 0))
        return out

    def row_sum(value):
        return jnp.sum(value, axis=1, keepdims=True)

    def coefficients(got, turn):
        gamma, delta, omega = unpack_dots(got)
        hist[...] = jnp.where(lane == turn, jnp.sqrt(omega / gamma), hist[...])
        gamma_prev = gprev[:, 0:1]
        alpha_prev = aprev[:, 0:1]
        beta = jnp.where(turn == 0, 0.0, gamma / gamma_prev)
        alpha = gamma / (delta - beta * gamma / alpha_prev)
        gprev[...] = jnp.broadcast_to(gamma, (cases, LANE))
        aprev[...] = jnp.broadcast_to(alpha, (cases, LANE))
        scal[...] = jnp.broadcast_to(beta, (cases, LANE))
        return alpha, beta

    def rows_of(c, buf):
        pieces = []
        for i in range(c * per_chunk, (c + 1) * per_chunk):
            value = vg[buf, i] * (rowpan[i, 3:4, :] * inv_root)
            top = value.astype(BF16)
            value = value - top.astype(F32)
            mid = value.astype(BF16)
            low = (value - mid.astype(F32)).astype(BF16)
            pieces.append(jnp.concatenate([top, mid, low], 0))
        return jnp.concatenate(pieces, 1)

    def product(lhs, top, low):
        main = jnp.dot(lhs, top, preferred_element_type=F32)
        rest = jnp.dot(lhs[:2 * cases], low, preferred_element_type=F32)
        small = main[2 * cases:] + rest[cases:]
        return main[:cases] + (main[cases:2 * cases] + rest[:cases] + small)

    def matmul(c, buf):
        part = product(rows_of(c, buf), ghi[c], glo[c])
        acc[...] = part if c == 0 else part + acc[...]

    def last_product(side_of):
        c = nchunk - 1
        cols = slice(side_of * cols_all, (side_of + 1) * cols_all)
        return acc[:, cols] + product(lhs_last[...], ghi[c, :, cols], glo[c, :, cols])

    def dots(first, stop, buf, parts):
        g, d, o = parts
        for i in range(first, stop):
            r, a = r_r[i], vg[buf, i]
            g, d, o = g + r * r, d + a * r, o + a * a
        return g, d, o

    def arrive(c, buf):
        with jax.named_scope(f"ag_wait{c}"):
            for k in order[c * per_chunk:(c + 1) * per_chunk]:
                ag_copy(k, buf).wait_recv()

    with jax.named_scope("build"):
        for c in range(nchunk):
            with jax.named_scope(f"pan_wait{c}"):
                for k in order[c * per_chunk:(c + 1) * per_chunk]:
                    pan_copy(k).wait_recv()
            if c > 0:
                arrive(c - 1, 0)
            build(c)
            if c > 0:
                matmul(c - 1, 0)
    partner_copy().wait_send()
    for k in every_chip:
        pan_copy(k).wait_send()

    def event(e, carry):
        par = lax.rem(e, 2)
        nxt = 1 - par
        buf = lax.rem(e, 3)
        after = lax.rem(e + 1, 3)
        @pl.when(e > 0)
        def _():
            for c in range(nchunk - 1):
                arrive(c, buf)
                with jax.named_scope(f"matmul{c}"):
                    matmul(c, buf)
                    parts = (sums[0], sums[1], sums[2])
                    if c == 0:
                        parts = (jnp.zeros((cases, LANE), F32),) * 3
                    sums[0], sums[1], sums[2] = dots(c * per_chunk, (c + 1) * per_chunk, buf, parts)
        arrive(nchunk - 1, buf)
        with jax.named_scope("last_A"):
            lhs_last[...] = rows_of(nchunk - 1, buf)
            part = last_product(0)
            for s in range(np_):
                px[s] = part[:, s * LANE:(s + 1) * LANE]
            parts = dots((nchunk - 1) * per_chunk, nslot, buf, (sums[0], sums[1], sums[2]))
            dots_out[...] = pack_dots([row_sum(v) for v in parts])
        px_copy(par).start()

        @pl.when(e >= 2)
        def _():
            for d, core in dot_peers:
                dt_copy(d, core, par).start()
        with jax.named_scope("last_B"):
            part = last_product(1)
            for s in range(np_):
                ps[s] = part[:, s * LANE:(s + 1) * LANE]
        dots_in[par, 0] = dots_out[...]
        with jax.named_scope("px_wait"):
            px_copy(par).wait_recv()
        for d in far_z + [0]:
            to = z_of(d)
            ps[to] = ps[to] + px_in[par, to]
            rs_copy(d, par).start()
        px_copy(par).wait_send()
        for k in every_chip:
            ag_copy(k, buf).wait_send()

        @pl.when(e > 0)
        def _():
            for d in far_z:
                zg_send(d, par).wait_send()
            cz[par, p] = vp[...]
        with jax.named_scope("rs_wait"):
            @pl.when(e >= 2)
            def _():
                for d, core in dot_peers:
                    dt_copy(d, core, par).wait_recv()
            for d in far_z + [0]:
                rs_copy(d, par).wait_recv()
        got = jnp.sum(rs[par], axis=0)
        fresh = got * panels[3:4, own] + diagonal[0:1, own] * vp[...]

        @pl.when(e == 0)
        def _():
            vp[...] = right[:, own] - fresh

        @pl.when(e == 1)
        def _():
            vp[...] = fresh

        @pl.when(e >= 2)
        def _():
            alpha, beta = coefficients(jnp.sum(dots_in[par], axis=0), e - 2)
            z = fresh + beta * zdir[...]
            zdir[...] = z
            vp[...] = vp[...] - alpha * z

        @pl.when(e < ITERS)
        def _():
            send_piece(after)
        for d in far_z:
            zg_send(d, nxt).start()
        with jax.named_scope("rs_send"):
            for d in far_z + [0]:
                rs_copy(d, par).wait_send()

        @pl.when(e >= 2)
        def _():
            for d, core in dot_peers:
                dt_copy(d, core, par).wait_send()

        @pl.when(e > 0)
        def _():
            for d in far_z:
                zg_recv(d, par).wait_recv()

        @pl.when(e == 1)
        def _():
            loop(0, nslot, lambda s: r_r.__setitem__(s, vg[buf, s]))
            loop(0, np_, lambda s: r_c.__setitem__(s, cz[par, s]))

        @pl.when(e >= 2)
        def _():
            alpha = aprev[...]
            beta = scal[...]

            def rows(s):
                step = vg[buf, s] + beta * s_r[s]
                s_r[s] = step
                r_r[s] = r_r[s] - alpha * step
            loop(0, nslot, rows)

            def cols(s):
                step = cz[par, s] + beta * s_c[s]
                s_c[s] = step
                along = r_c[s] + beta * d_c[s]
                d_c[s] = along
                sol_c[s] = sol_c[s] + alpha * along
                r_c[s] = r_c[s] - alpha * step
            loop(0, np_, cols)
        return carry

    lax.fori_loop(0, ITERS + 1, event, 0)

    last = (ITERS + 1) % 2
    r = r_c[p]
    a = vp[...]
    dtile[...] = pack_dots([row_sum(r * r), row_sum(a * r), row_sum(a * a)])
    for k, core in reversed(everyone):
        plane_copy(k, core).start()
    dplane[0] = dtile[...]
    cz[last, p] = vp[...]
    with jax.named_scope("dp_wait"):
        for k, core in everyone:
            plane_copy(k, core).wait_recv()
    dsum[...] = jnp.sum(dplane[...], axis=0)
    for d in far_z:
        dz_copy(d).start()
    dz[0] = dsum[...]
    for k, core in everyone:
        plane_copy(k, core).wait_send()
    for d in far_z:
        zg_send(d, last).wait_send()
    with jax.named_scope("dz_wait"):
        for d in far_z:
            zg_recv(d, last).wait_recv()
        for d in far_z:
            dz_copy(d).wait_recv()
    alpha, beta = coefficients(jnp.sum(dz[...], axis=0), ITERS - 1)
    for s in range(np_):
        cols = slice(s * LANE, (s + 1) * LANE)
        step = cz[last, s] + beta * s_c[s]
        along = r_c[s] + beta * d_c[s]
        sol_out[:, cols] = sol_c[s] + alpha * along
        res_out[:, cols] = r_c[s] - alpha * step
    hist_out[...] = hist[...].T[0:ITERS, :]
    for d in far_z:
        dz_copy(d).wait_send()


def hand_over(*refs):
    n = (len(refs) - 1) // 3
    src, dst, mid, sems = refs[:n], refs[n:2 * n], refs[2 * n:3 * n], refs[3 * n]
    loads = [pltpu.make_async_copy(src[i], mid[i], sems.at[0, i]) for i in range(n)]
    stores = [pltpu.make_async_copy(mid[i], dst[i], sems.at[1, i]) for i in range(n)]
    for load in loads:
        load.start()
    for load, store in zip(loads, stores):
        load.wait()
        store.start()
    for store in stores:
        store.wait()


def on_device(np_, ngy, panels, diagonal, right, start):
    cases, cols = right.shape
    nslot = ngy
    per_chunk = nslot // 4
    span = LANE * per_chunk
    parts = nslot // per_chunk
    vm = lambda *shape: pltpu.VMEM(shape, F32)
    half = lambda *shape: pltpu.VMEM(shape, BF16)
    dma = lambda *shape: pltpu.SemaphoreType.DMA(shape)
    state = (np_, cases, LANE)
    wide = (nslot, cases, LANE)
    one = (cases, LANE)
    scratch = [
        vm(4, cols), vm(4, cols), vm(1, cols), vm(cases, cols), vm(cases, cols), vm(nslot, 4, LANE),
        half(parts, span, 2 * cols), half(parts, span, 2 * cols), half(48, 2 * cols), half(3 * cases, span),
        vm(*one), vm(3, *wide), vm(2, *state), vm(*state), vm(2, *state), vm(*state), vm(2, *state),
        vm(8, LANE), vm(2, 2 * np_, 8, LANE), vm(cases, 2 * cols),
        vm(*state), vm(*state), vm(*state), vm(*state), vm(*wide), vm(*wide),
        vm(*one), vm(*one), vm(*one), vm(*one), vm(*one), vm(3, *one),
        vm(8, LANE), vm(2 * nslot, 8, LANE), vm(8, LANE), vm(np_, 8, LANE),
        dma(5), dma(nslot), dma(nslot), pltpu.SemaphoreType.DMA, pltpu.SemaphoreType.DMA,
        dma(nslot), dma(3, nslot), dma(np_), dma(2, np_), pltpu.SemaphoreType.DMA, dma(2),
        dma(np_), dma(2, np_), dma(2 * np_), dma(2, 2 * np_),
        dma(2 * nslot), dma(2 * nslot), dma(np_), dma(np_),
    ]
    results = pl.pallas_call(
        functools.partial(cg_kernel, np_, ngy, cases, per_chunk),
        out_shape=(
            jax.ShapeDtypeStruct((cases, cols), F32),
            jax.ShapeDtypeStruct((cases, cols), F32),
            jax.ShapeDtypeStruct((ITERS, cases), F32),
        ),
        in_specs=[pl.BlockSpec(memory_space=pltpu.HBM)] * 4,
        out_specs=tuple([pl.BlockSpec(memory_space=pltpu.VMEM)] * 3),
        scratch_shapes=scratch,
        compiler_params=pltpu.CompilerParams(
            collective_id=0, has_side_effects=True, vmem_limit_bytes=60 * 1024 * 1024
        ),
        name="cg",
    )(panels, diagonal[None, :], right, start)
    return pl.pallas_call(
        hand_over,
        out_shape=tuple(jax.ShapeDtypeStruct(r.shape, r.dtype) for r in results),
        in_specs=[pl.BlockSpec(memory_space=pltpu.HBM)] * 3,
        out_specs=tuple([pl.BlockSpec(memory_space=pltpu.HBM)] * 3),
        scratch_shapes=[pltpu.VMEM(r.shape, r.dtype) for r in results] + [pltpu.SemaphoreType.DMA((2, 3))],
        compiler_params=pltpu.CompilerParams(vmem_limit_bytes=60 * 1024 * 1024),
        name="hand_over",
    )(*results)


def solution(mesh):
    cut = P(None, ("gy", "gz"))
    sizes = dict(mesh.shape)
    return jax.shard_map(
        functools.partial(on_device, sizes["gx"], sizes["gy"]),
        mesh=mesh,
        in_specs=(cut, P(("gy", "gz")), cut, cut),
        out_specs=(cut, cut, P()),
        check_vma=False,
    )
```

time: 106 us -> 99.4 us (0.938)
  Pallas kernels: 102 us -> 98.5 us
  local copies, waits for them, and re-layouts: 2.86 us -> 0 us
    pallas_call x1, Pallas kernels: 102 us -> 96.9 us  [on_device(): pl.pallas_call(functools.partial(cg_kernel, np_, ngy, cases, per_chunk),...]
    unnamed x7 -> x0, local copies, waits for them, and re-layouts: 2.86 us -> none
    pallas_call x0 -> x1, Pallas kernels: none -> 1.68 us  [on_device(): pl.pallas_call(hand_over, out_shape=tuple((jax.ShapeDtypeStruct(r.shape,...]
where the time goes in v3:
time: 99.4 us; the launch traced here: 99.2 us
  Pallas kernels  98.5 us (99%)
    pallas_call x1, Pallas kernels, on_device(): pl.pallas_call(functools.partial(cg_kernel, np_, ngy, cases, per_chunk),...  96.9 us

profile of v3, /device:TPU:1, one launch (start us, length us, event | category | flops | bytes accessed | tf_op | source)
XLA Modules:
  0.0 99.2 jit_solution(2500914483252618017)
XLA Ops:
  0.6 96.9 %cg.1 = (f32[32,1024]{1,0:T(8,128)}, f32[32,1024]{1,0:T(8,128)}, f32[4,32]{1,0:T(4,128)}) custom-call(f32[4,1024]{1,0:T(4,128)} %panels_hbm.1, f32[1,1024]{1,0:T(1,128)} %bitcast.1, f32[32,1024]{1,0:T(8,128)} %right_hbm.1, f32[32,1024]{1,0:T(8,128)} %start_hbm.1), custom_call_target="tpu_custom_call" | custom-call | tf_op jit(solution)/shard_map/cg/pallas_call | solution.py:479
  97.5 1.7 %hand_over.1 = (f32[32,1024]{1,0:T(8,128)}, f32[32,1024]{1,0:T(8,128)}, f32[4,32]{1,0:T(4,128)}) custom-call(f32[32,1024]{1,0:T(8,128)} %get-tuple-element.6.refs_0_, f32[32,1024]{1,0:T(8,128)} %get-tuple-element.7.refs_1_, f32[4,32]{1,0:T(4,128)} %get-tuple-element.8.refs_2_), custom_call_target="tpu_custom_call" | custom-call | tf_op jit(solution)/shard_map/hand_over/pallas_call | solution.py:494
